TPU v7x, 32 devices: a whole 2x2x4 slice. The times are simulated.
32 devices in a mesh: tok: 2 (over x), vocab: 16 (over z, y, core).
Axes of the slice: x: 2, y: 2, z: 4, core: 2. Of those that a mesh axis runs over, the one named last changes fastest.
Arguments:
- hidden: bfloat16 [1536, 4096], P('tok', 'vocab'), as said below
- weight: bfloat16 [4096, 16384], P('tok', 'vocab'), may hold values from -0.09375 to 0.09375
- targets: int32 [1536], P('tok'), may hold values from 0 to 16383
- domains: int32 [1536], P('tok'), may hold values from 0 to 63
- seq_len: int32 [12], P('tok'), may hold values from 1 to 128
Outputs:
- token_loss: float32 [1536], P(('tok', 'vocab'))
- domain_mean: float32 [64], replicated
Inputs may be any that keep to these rules, and one draw needn't show every extreme that they name: hidden states of the eval window.
All inputs are finite; a program needn't handle non-finite values.
Results may differ from a plain program's by a relative error of at most 0.0003.
Values may be sent and summed in bfloat16 or wider, within the bound.
A program may use at most 64 MiB of HBM per device.

v0:
```python
import jax
import jax.numpy as jnp
from jax import lax
from jax.sharding import PartitionSpec as P

SEQ_LEN = 128
DOMAINS = 64


def body(hidden, weight, targets, domains, seq_len):
    features = lax.all_gather(hidden, "vocab", axis=1, tiled=True)
    tok_rows = features.shape[0]
    columns = weight.shape[1]
    logits = jnp.dot(
        features,
        lax.all_gather(weight, "tok", axis=0, tiled=True),
        preferred_element_type=jnp.float32,
    )
    first_col = lax.axis_index("vocab") * columns
    column_ids = first_col + lax.broadcasted_iota(jnp.int32, (tok_rows, columns), 1)
    picked_loc = jnp.sum(jnp.where(column_ids == targets[:, None], logits, 0.0), axis=1)
    top_loc = jnp.max(logits, axis=1)
    groups = lax.axis_size("vocab")
    share_len = tok_rows // groups
    share_start = lax.axis_index("vocab") * share_len
    sum_loc = jnp.sum(jnp.exp(logits - top_loc[:, None]), axis=1)
    gathered = (
        lax.all_to_all(
            top_loc.reshape(groups, share_len), "vocab", split_axis=0, concat_axis=0, tiled=True
        ),
        lax.all_to_all(
            sum_loc.reshape(groups, share_len), "vocab", split_axis=0, concat_axis=0, tiled=True
        ),
        lax.all_to_all(
            picked_loc.reshape(groups, share_len), "vocab", split_axis=0, concat_axis=0, tiled=True
        ),
    )
    row_top = jnp.max(gathered[0], axis=0)
    row_total = jnp.sum(gathered[1] * jnp.exp(gathered[0] - row_top[None, :]), axis=0)
    picked = jnp.sum(gathered[2], axis=0)
    loss_raw = jnp.log(row_total) + row_top - picked
    positions = share_start + lax.iota(jnp.int32, share_len)
    seq_ids = positions // SEQ_LEN
    seq_count = seq_len.shape[0]
    lengths = jnp.sum(
        jnp.where(
            seq_ids[:, None] == lax.broadcasted_iota(jnp.int32, (share_len, seq_count), 1),
            seq_len[None, :],
            0,
        ),
        axis=1,
    )
    valid_mask = (positions % SEQ_LEN < lengths).astype(jnp.float32)
    token_loss = loss_raw * valid_mask
    domain_share = lax.dynamic_slice_in_dim(domains, share_start, share_len)
    onehot = (
        domain_share[:, None] == lax.broadcasted_iota(jnp.int32, (share_len, DOMAINS), 1)
    ).astype(jnp.float32)
    domain_sum = jnp.dot(token_loss, onehot, precision=lax.Precision.HIGHEST)
    domain_count = jnp.dot(valid_mask, onehot, precision=lax.Precision.HIGHEST)
    domain_sum, domain_count = lax.psum((domain_sum, domain_count), ("tok", "vocab"))
    domain_mean = domain_sum / jnp.maximum(domain_count, 1.0)
    return (token_loss, domain_mean)


def solution(mesh):
    in_specs = (P("tok", "vocab"), P("tok", "vocab"), P("tok"), P("tok"), P("tok"))
    out_specs = (P(("tok", "vocab")), P())
    return jax.shard_map(body, mesh=mesh, in_specs=in_specs, out_specs=out_specs, check_vma=False)
```

profile of v0, /device:TPU:0, one launch (start us, length us, event | category | flops | bytes accessed | tf_op | source)
XLA Modules:
  0.0 270.7 jit_solution(16608660790201364310)
XLA Ops:
  7.2 0.0 all-gather.5.cloned.1.call-start
  7.2 0.7 all-gather.5.cloned.1.call-update
  7.9 0.0 all-gather.3.cloned.1.call-start
  7.9 0.7 all-gather.3.cloned.1.call-update
  8.7 0.0 copy-start
  8.7 107.6 %all-gather.5.cloned.1.call-done = bf16[4096,1024]{1,0:T(8,128)(2,1)} async-done(((bf16[2048,1024]{1,0:T(8,128)(2,1)}), bf16[4096,1024]{1,0:T(8,128)(2,1)}) %all-gather.5.cloned.1.call-update) | async-done | bytes 8388624 | tf_op jit(solution)/shard_map/all_gather | solution.py:16
  116.2 67.4 %all-gather.3.cloned.1.call-done = bf16[768,4096]{1,0:T(8,128)(2,1)} async-done(((bf16[768,256]{1,0:T(8,128)(2,1)}), bf16[768,4096]{1,0:T(8,128)(2,1)}) %all-gather.3.cloned.1.call-update) | async-done | bytes 6291472 | tf_op jit(solution)/shard_map/all_gather | solution.py:11
  183.7 11.1 %fusion.6 = (f32[768]{0:T(1024)S(1)}, f32[768,1024]{1,0:T(8,128)S(1)}) fusion(bf16[768,4096]{1,0:T(8,128)(2,1)} %all-gather.3.cloned.1.call-done, bf16[4096,1024]{1,0:T(8,128)(2,1)} %all-gather.5.cloned.1.call-done), kind=kOutput, calls=%fused_computation.22 | convolution fusion | flops 6443236352 | bytes 17828864 | tf_op jit(solution)/shard_map/dot_general | solution.py:14
  194.8 0.0 copy-start.2
  194.8 0.7 all_to_all.25
  195.4 3.4 %all-to-all-start.1 = ((f32[16,1,48]{2,1,0:T(1,128)}), f32[16,1,48]{2,1,0:T(1,128)S(1)}, u32[]{:S(2)}, u32[]{:S(2)}) async-start(f32[16,1,48]{2,1,0:T(1,128)} %all_to_all.25), calls=%async_computation.1 | async-start | bytes 16384 | tf_op jit(solution)/shard_map/all_to_all | solution.py:28
  198.9 0.0 copy-done
  198.9 0.9 exponential_reduce_fusion
  199.8 0.7 all_to_all.28
  200.5 4.8 %all-to-all-done.1 = f32[16,1,48]{2,1,0:T(1,128)S(1)} async-done(((f32[16,1,48]{2,1,0:T(1,128)}), f32[16,1,48]{2,1,0:T(1,128)S(1)}, u32[]{:S(2)}, u32[]{:S(2)}) %all-to-all-start.1) | async-done | bytes 3104 | tf_op jit(solution)/shard_map/all_to_all | solution.py:28
  205.3 3.5 %all-to-all-start.2 = ((f32[16,1,48]{2,1,0:T(1,128)}), f32[16,1,48]{2,1,0:T(1,128)S(1)}, u32[]{:S(2)}, u32[]{:S(2)}) async-start(f32[16,1,48]{2,1,0:T(1,128)} %all_to_all.28), calls=%async_computation.2 | async-start | bytes 16384 | tf_op jit(solution)/shard_map/all_to_all | solution.py:34
  208.8 0.0 copy-done.2
  208.8 0.1 select_reduce_fusion.1
  208.9 0.8 dynamic_slice.3
  209.6 0.7 all_to_all.22
  210.3 4.9 %all-to-all-done.2 = f32[16,1,48]{2,1,0:T(1,128)S(1)} async-done(((f32[16,1,48]{2,1,0:T(1,128)}), f32[16,1,48]{2,1,0:T(1,128)S(1)}, u32[]{:S(2)}, u32[]{:S(2)}) %all-to-all-start.2) | async-done | bytes 3104 | tf_op jit(solution)/shard_map/all_to_all | solution.py:34
  215.2 3.4 %all-to-all-start = ((f32[16,1,48]{2,1,0:T(1,128)}), f32[16,1,48]{2,1,0:T(1,128)S(1)}, u32[]{:S(2)}, u32[]{:S(2)}) async-start(f32[16,1,48]{2,1,0:T(1,128)} %all_to_all.22), calls=%async_computation | async-start | bytes 16384 | tf_op jit(solution)/shard_map/all_to_all | solution.py:31
  218.6 0.2 convolution_bitcast_fusion
  218.8 6.1 %all-to-all-done = f32[16,1,48]{2,1,0:T(1,128)S(1)} async-done(((f32[16,1,48]{2,1,0:T(1,128)}), f32[16,1,48]{2,1,0:T(1,128)S(1)}, u32[]{:S(2)}, u32[]{:S(2)}) %all-to-all-start) | async-done | bytes 3104 | tf_op jit(solution)/shard_map/all_to_all | solution.py:31
  225.0 0.0 copy-start.1
  225.0 0.2 convolution_bitcast_fusion.1
  225.2 38.2 %all-reduce = (f32[64]{0:T(128)S(1)}, f32[64]{0:T(128)S(1)}) all-reduce(f32[64]{0:T(128)S(1)} %convolution_bitcast_fusion.1, f32[64]{0:T(128)S(1)} %convolution_bitcast_fusion), channel_id=1, replica_groups=mesh['tok'=2,'vocab'=16] {'tok','vocab'}, use_global_device_ids=true, to_apply=%region_7.8 | all-reduce | flops 128 | bytes 1024 | tf_op jit(solution)/shard_map/psum | solution.py:61
  263.4 0.5 maximum_divide_fusion
  263.9 0.0 copy-done.1
  (6 shorter events, 0.1 us)
Async XLA Ops:
  7.2 109.1 %all-gather.5.cloned.1.call-start = ((), (), s32[]{:S(2)}) async-start(), calls=%async_computation.4 | async-start | bytes 12582912 | tf_op jit(solution)/shard_map/all_gather | solution.py:16
  7.9 175.8 %all-gather.3.cloned.1.call-start = ((), (), s32[]{:S(2)}) async-start(), calls=%async_computation.3 | async-start | bytes 6684672 | tf_op jit(solution)/shard_map/all_gather | solution.py:11
  8.7 190.2 %copy-start = (s32[768]{0:T(1024)S(1)}, s32[768]{0:T(1024)}, u32[]{:S(2)}) copy-start(s32[768]{0:T(1024)} %param.7) | copy-start | bytes 9220
  194.8 14.0 %copy-start.2 = (s32[6]{0:T(128)S(1)}, s32[6]{0:T(128)}, u32[]{:S(2)}) copy-start(s32[6]{0:T(128)} %param.9) | copy-start | bytes 76
  195.4 9.8 %all-to-all-start.1 = ((f32[16,1,48]{2,1,0:T(1,128)}), f32[16,1,48]{2,1,0:T(1,128)S(1)}, u32[]{:S(2)}, u32[]{:S(2)}) async-start(f32[16,1,48]{2,1,0:T(1,128)} %all_to_all.25), calls=%async_computation.1 | async-start | bytes 16384 | tf_op jit(solution)/shard_map/all_to_all | solution.py:28
  205.3 9.9 %all-to-all-start.2 = ((f32[16,1,48]{2,1,0:T(1,128)}), f32[16,1,48]{2,1,0:T(1,128)S(1)}, u32[]{:S(2)}, u32[]{:S(2)}) async-start(f32[16,1,48]{2,1,0:T(1,128)} %all_to_all.28), calls=%async_computation.2 | async-start | bytes 16384 | tf_op jit(solution)/shard_map/all_to_all | solution.py:34
  215.2 9.8 %all-to-all-start = ((f32[16,1,48]{2,1,0:T(1,128)}), f32[16,1,48]{2,1,0:T(1,128)S(1)}, u32[]{:S(2)}, u32[]{:S(2)}) async-start(f32[16,1,48]{2,1,0:T(1,128)} %all_to_all.22), calls=%async_computation | async-start | bytes 16384 | tf_op jit(solution)/shard_map/all_to_all | solution.py:31
  225.0 38.9 %copy-start.1 = (f32[48]{0:T(128)}, f32[48]{0:T(128)S(1)}, u32[]{:S(2)}) copy-start(f32[48]{0:T(128)S(1)} %subtract_select_fusion) | copy-start | bytes 580
Sparse Core Ops, SparseCore 0:
  9.5 106.6 all-gather.4
  118.4 65.2 all-gather.2
where the time goes:
time: 271 us
  waiting for transfers between devices  192 us (71%)
  blocking collectives  38.2 us (14%)
  between operations  14.1 us (5%)
  matrix products  11.4 us (4%)
  starting transfers between devices  10.4 us (4%)
  local copies, waits for them, and re-layouts  2.8 us (1%)
    all_gather x1, waiting for transfers between devices, body(): lax.all_gather(weight, 'tok', axis=0, tiled=True)  108 us
    all_gather x1, waiting for transfers between devices, body(): features = lax.all_gather(hidden, 'vocab', axis=1, tiled=True)  67.4 us
    psum x1, blocking collectives, body(): lax.psum((domain_sum, domain_count), ('tok', 'vocab'))  38.2 us
    dot_general x1, matrix products, body(): jnp.dot(features, lax.all_gather(weight, 'tok', axis=0, tiled=True), pref...  11.1 us
    all_to_all x1, waiting for transfers between devices, body(): lax.all_to_all(sum_loc.reshape(groups, share_len), 'vocab', split_axis=0,...  6.14 us
  transfers between devices with their start and end apart: 5, of which 5 were waited for; matrix products, arithmetic and copies ran while one was open for 1% of the time, Pallas kernels for 0%

commit v1 on v0

v1 whole, which is shorter than its diff:
```python
import functools

import jax
import jax.numpy as jnp
from jax import lax
from jax.experimental import pallas as pl
from jax.experimental.pallas import tpu as pltpu
from jax.sharding import PartitionSpec as P

SEQ_LEN = 128
DOMAINS = 64
LANES = 128
TILE = 8
GATHER_LIMIT = 24 << 20
MESH = pl.DeviceIdType.MESH


def body(hidden, weight, targets, domains, seq_len):
    features = lax.all_gather(hidden, "vocab", axis=1, tiled=True)
    tok_rows = features.shape[0]
    columns = weight.shape[1]
    logits = jnp.dot(
        features,
        lax.all_gather(weight, "tok", axis=0, tiled=True),
        preferred_element_type=jnp.float32,
    )
    first_col = lax.axis_index("vocab") * columns
    column_ids = first_col + lax.broadcasted_iota(jnp.int32, (tok_rows, columns), 1)
    picked_loc = jnp.sum(jnp.where(column_ids == targets[:, None], logits, 0.0), axis=1)
    top_loc = jnp.max(logits, axis=1)
    groups = lax.axis_size("vocab")
    share_len = tok_rows // groups
    sum_loc = jnp.sum(jnp.exp(logits - top_loc[:, None]), axis=1)
    gathered = [
        lax.all_to_all(
            part.reshape(groups, share_len), "vocab", split_axis=0, concat_axis=0, tiled=True
        )
        for part in (top_loc, sum_loc, picked_loc)
    ]
    row_top = jnp.max(gathered[0], axis=0)
    row_total = jnp.sum(gathered[1] * jnp.exp(gathered[0] - row_top[None, :]), axis=0)
    picked = jnp.sum(gathered[2], axis=0)
    loss_raw = jnp.log(row_total) + row_top - picked
    valid_mask, domain_share = token_share(domains, seq_len, share_len)
    token_loss = loss_raw * valid_mask
    onehot = (
        domain_share[:, None] == lax.broadcasted_iota(jnp.int32, (share_len, DOMAINS), 1)
    ).astype(jnp.float32)
    domain_sum = jnp.dot(token_loss, onehot, precision=lax.Precision.HIGHEST)
    domain_count = jnp.dot(valid_mask, onehot, precision=lax.Precision.HIGHEST)
    domain_sum, domain_count = lax.psum((domain_sum, domain_count), ("tok", "vocab"))
    domain_mean = domain_sum / jnp.maximum(domain_count, 1.0)
    return (token_loss, domain_mean)


def token_share(domains, seq_len, share_len):
    share_start = lax.axis_index("vocab") * share_len
    positions = share_start + lax.iota(jnp.int32, share_len)
    seq_ids = positions // SEQ_LEN
    seq_count = seq_len.shape[0]
    lengths = jnp.sum(
        jnp.where(
            seq_ids[:, None] == lax.broadcasted_iota(jnp.int32, (share_len, seq_count), 1),
            seq_len[None, :],
            0,
        ),
        axis=1,
    )
    valid_mask = (positions % SEQ_LEN < lengths).astype(jnp.float32)
    return valid_mask, lax.dynamic_slice_in_dim(domains, share_start, share_len)


@functools.lru_cache(None)
def plan(depth):
    queues = {}
    have = [dict() for _ in range(depth)]
    for z in range(depth):
        have[z][(0, 0, z)] = 0.0
        have[z][(1, 0, z)] = 1.0
    pending = [(have[z][s], z, s) for z in range(depth) for s in have[z]]
    free = {}
    sends = [dict() for _ in range(depth)]

    def push(now, z, link, shard):
        start = max(now, free.get((z, link), 0.0))
        free[(z, link)] = start + 1.0
        to, item = {
            "y": (z, (shard[0], 1, shard[2])),
            "up": (z + 1, shard),
            "down": (z - 1, shard),
        }[link]
        have[to][item] = start + 1.0
        pending.append((start + 1.0, to, item))
        sends[z].setdefault(shard, []).append(link)

    while pending:
        pending.sort()
        now, z, shard = pending.pop(0)
        sends[z].setdefault(shard, [])
        if shard[1]:
            continue
        if z < depth - 1 and shard[2] <= z:
            push(now, z, "up", shard)
        if z > 0 and shard[2] >= z:
            push(now, z, "down", shard)
        if not (shard[0] == 0 and shard[2] == (z ^ 1)):
            push(now, z, "y", shard)
    for z in range(depth):
        link = "up" if z % 2 == 0 else "down"
        start = max(have[z][(0, 1, z)], free[(z, link)])
        have[z ^ 1][(0, 1, z)] = start + 1.0
    order = []
    for z in range(depth):
        link = "up" if z % 2 == 0 else "down"
        events = sorted((time, shard) for shard, time in have[z].items())
        after = max(
            [i for i, (_, s) in enumerate(events) if link in sends[z].get(s, ())]
            + [i for i, (_, s) in enumerate(events) if s == (0, 1, z)]
        )
        rows = []
        for i, (time, shard) in enumerate(events):
            links = list(sends[z].get(shard, []))
            rows.append((time, shard, links + (["far"] if i == after else [])))
        order.append(rows)
    return order


@functools.lru_cache(None)
def program(depth):
    order = plan(depth)
    pieces = 4 * depth // 2
    weight_order, products = {}, {}
    for t in range(2):
        for z in range(depth):
            arrival = {s: time for time, s, _ in order[z]}
            remote = [zz for zz in range(depth) if zz // (depth // 2) != t]
            remote.sort(key=lambda zz: (abs(zz - z), zz))
            chunks = [(zz, dy, dc) for zz in remote for dy in range(2) for dc in range(2)]
            weight_order[(t, z)] = chunks
            at = {ch: 1.0 + (i + 1) * 16.0 / 3 / pieces for i, ch in enumerate(chunks)}
            ready = []
            for zz in range(depth):
                for dy in range(2):
                    for dc in range(2):
                        time = max(arrival[(0, dy, zz)], arrival[(1, dy, zz)]) + 0.15 * dc
                        ready.append((max(time, at.get((zz, dy, dc), 0.0)), (zz, dy, dc)))
            products[(t, z)] = sorted(ready)
    keys = sorted(products)
    count = len(order[0])
    steps = [
        (sum(order[z][i][0] for z in range(depth)) / depth, 0, i) for i in range(1, count)
    ]
    steps += [
        (sum(products[k][i][0] for k in keys) / len(keys) + 0.2, 1, i)
        for i in range(len(products[keys[0]]))
    ]
    steps.sort()
    arrived = {z: {order[z][0][1]} for z in range(depth)}
    sequence, waiting = [], []

    def ready_now(i):
        return all(
            products[k][i][1][2] == 1
            or {(0,) + products[k][i][1][1::-1], (1,) + products[k][i][1][1::-1]}
            <= arrived[k[1]]
            for k in keys
        )

    for _, kind, i in steps:
        if kind == 0:
            sequence.append((0, i))
            for z in range(depth):
                arrived[z].add(order[z][i][1])
        else:
            waiting.append(i)
        while waiting and ready_now(waiting[0]):
            sequence.append((1, waiting.pop(0)))
    assert not waiting
    return order, weight_order, products, sequence


def kernel(
    depth, hid, weight, tgt, dom, mask, loss_out, mean_out,
    held, wts, acc, tgt_all, tgt_col, stat, stat_in, part, part_in,
    own_sem, held_sem, wts_sem, send_sem, wsend_sem, tgt_sem,
    s1_send, s1_recv, s2_send, s2_recv,
):
    order, weight_order, products, sequence = program(depth)
    t, v = lax.axis_index("tok"), lax.axis_index("vocab")
    vocab = 4 * depth
    devices = 2 * vocab
    me = t * vocab + v
    z, y, c = v // 4, (v // 2) % 2, v % 2
    tok_rows, kb = hid.shape
    cols = wts.shape[2]
    locals_ = vocab // 2
    share = tok_rows // vocab

    def sel(values, index):
        if all(a == values[0] for a in values):
            return values[0]
        out = jnp.int32(values[0])
        for i, a in enumerate(values[1:], 1):
            out = jnp.where(index == i, jnp.int32(a), out)
        return out

    key = t * depth + z

    own = pltpu.make_async_copy(hid, held.at[t, v], own_sem.at[0])
    own.start()
    own_tgt = pltpu.make_async_copy(tgt, tgt_all.at[t], own_sem.at[1])
    own_tgt.start()

    def mine(r):
        return pltpu.make_async_copy(
            weight.at[pl.ds(r * kb, kb), pl.ds(pl.multiple_of(t * cols, LANES), cols)],
            wts.at[t * locals_ + r],
            wts_sem.at[t * locals_ + r],
        )

    for r in range(locals_):
        mine(r).start()

    barrier = pltpu.get_barrier_semaphore()

    def greet(k, carry):
        other = (me + k) % devices
        pl.semaphore_signal(
            barrier, inc=1, device_id=(other // vocab, other % vocab), device_id_type=MESH
        )
        return carry

    lax.fori_loop(1, devices, greet, 0)
    own.wait()
    own_tgt.wait()
    pl.semaphore_wait(barrier, devices - 1)

    where = {
        "x": lambda: (1 - t, v),
        "y": lambda: (t, v + 2 - 4 * y),
        "up": lambda: (t, v + 4),
        "down": lambda: (t, v - 4),
        "far": lambda: (t, v + 4 - 8 * (z % 2)),
        "pair": lambda: (t, v + 1 - 2 * c),
    }
    lanes_of = {"x": 0, "y": 1, "up": 2, "down": 3, "far": 4, "pair": 5}
    sent = []

    def send(tt, vv, link, step, places):
        copy = pltpu.make_async_remote_copy(
            src_ref=held.at[tt, vv],
            dst_ref=held.at[tt, vv],
            send_sem=send_sem.at[step, lanes_of[link]],
            recv_sem=held_sem.at[tt, vv],
            device_id=where[link](),
            device_id_type=MESH,
        )
        guarded(places, copy.start)
        sent.append((places, copy))

    def guarded(places, act):
        if len(places) == depth:
            act()
            return
        hit = z == places[0]
        for p in places[1:]:
            hit = jnp.logical_or(hit, z == p)
        pl.when(hit)(act)

    def fan_out(step):
        tt = (t + sel([order[p][step][1][0] for p in range(depth)], z)) % 2
        yy = (y + sel([order[p][step][1][1] for p in range(depth)], z)) % 2
        zz = sel([order[p][step][1][2] for p in range(depth)], z)
        vv = zz * 4 + yy * 2 + c
        if step:
            pltpu.make_async_copy(hid, held.at[tt, vv], held_sem.at[tt, vv]).wait()
        if not step:
            send(tt, vv, "x", 0, list(range(depth)))
        for link in ("up", "down", "y"):
            places = [p for p in range(depth) if link in order[p][step][2]]
            if places:
                send(tt, vv, link, step, places)
        send(tt, vv, "pair", step, list(range(depth)))
        places = [p for p in range(depth) if "far" in order[p][step][2]]
        if places:
            send(t, z * 4 + (1 - y) * 2 + c, "far", step, places)

    fan_out(0)
    tgt_copy = pltpu.make_async_remote_copy(
        src_ref=tgt_all.at[t], dst_ref=tgt_all.at[t],
        send_sem=tgt_sem.at[0], recv_sem=tgt_sem.at[1],
        device_id=where["x"](), device_id_type=MESH,
    )
    tgt_copy.start()

    wsent = []
    for i in range(locals_):
        chunk = [weight_order[(1 - k // depth, k % depth)][i] for k in range(2 * depth)]
        zz = sel([ch[0] for ch in chunk], key)
        yy = (y + sel([ch[1] for ch in chunk], key)) % 2
        cc = (c + sel([ch[2] for ch in chunk], key)) % 2
        vv = zz * 4 + yy * 2 + cc
        row = pl.multiple_of((vv - t * locals_) * kb, kb)
        copy = pltpu.make_async_remote_copy(
            src_ref=weight.at[pl.ds(row, kb), pl.ds(pl.multiple_of((1 - t) * cols, LANES), cols)],
            dst_ref=wts.at[vv],
            send_sem=wsend_sem.at[i],
            recv_sem=wts_sem.at[vv],
            device_id=where["x"](),
            device_id_type=MESH,
        )
        copy.start()
        wsent.append(copy)

    tgt_copy.wait()

    def spread(i, carry):
        for h in range(2):
            row = tgt_all[h, pl.ds(i, 1), :].astype(jnp.float32)
            tgt_col[pl.ds(pl.multiple_of(h * tok_rows + i * LANES, LANES), LANES), :] = jnp.transpose(
                jnp.broadcast_to(row, (LANES, LANES))
            )
        return carry

    lax.fori_loop(0, tok_rows // LANES, spread, 0)

    def product(i, first):
        chunk = [products[(k // depth, k % depth)][i][1] for k in range(2 * depth)]
        zz = sel([ch[0] for ch in chunk], key)
        yy = (y + sel([ch[1] for ch in chunk], key)) % 2
        dc = sel([ch[2] for ch in chunk], key)
        vv = zz * 4 + yy * 2 + (c + dc) % 2

        def wait_pair():
            for h in range(2):
                pltpu.make_async_copy(hid, held.at[h, vv], held_sem.at[h, vv]).wait()

        if isinstance(dc, int):
            if dc:
                wait_pair()
        else:
            pl.when(dc == 1)(wait_pair)
        pltpu.make_async_copy(wts.at[vv], wts.at[vv], wts_sem.at[vv]).wait()
        step_rows = 256 if tok_rows % 256 == 0 else LANES

        def tile(r, carry):
            for h in range(2):
                at = pl.ds(pl.multiple_of(r * step_rows, step_rows), step_rows)
                to = pl.ds(pl.multiple_of(h * tok_rows + r * step_rows, step_rows), step_rows)
                got = jnp.dot(held[h, vv, at, :], wts[vv], preferred_element_type=jnp.float32)
                if first:
                    acc[to, :] = got
                else:
                    acc[to, :] += got
            return carry

        lax.fori_loop(0, tok_rows // step_rows, tile, 0)

    first = True
    for kind, i in sequence:
        if kind == 0:
            fan_out(i)
        else:
            product(i, first)
            first = False

    first_col = (v * 2 + t) * cols
    lane = lax.broadcasted_iota(jnp.int32, (share, LANES), 1)
    col = lax.broadcasted_iota(jnp.int32, (share, cols), 1)

    def finish(w, carry):
        rows = pl.ds(pl.multiple_of(w * share, share), share)
        got = acc[rows, :]
        wanted = tgt_col[rows, 0:1].astype(jnp.int32) - first_col
        top = jnp.max(got, axis=1, keepdims=True)
        total = jnp.sum(jnp.exp(got - top), axis=1, keepdims=True)
        picked = jnp.sum(jnp.where(col == wanted, got, 0.0), axis=1, keepdims=True)
        both = jnp.where(lane == 0, top, jnp.where(lane == 1, total, picked))
        both = jnp.concatenate([both, jnp.zeros((LANES - share, LANES), jnp.float32)], axis=0)
        stat[w] = jnp.transpose(both)[:TILE, :]
        return carry

    lax.fori_loop(0, devices, finish, 0)

    def exchange(src_at, dst, send, recv):
        def copy(k):
            other = (me + k) % devices
            return pltpu.make_async_remote_copy(
                src_ref=src_at(other), dst_ref=dst.at[me],
                send_sem=send.at[other], recv_sem=recv.at[me],
                device_id=(other // vocab, other % vocab), device_id_type=MESH,
            )

        def go(k, carry):
            copy(k).start()
            return carry

        def done(k, carry):
            other = (me + k) % devices
            copy(k).wait_send()
            pltpu.make_async_copy(dst.at[other], dst.at[other], recv.at[other]).wait()
            return carry

        lax.fori_loop(1, devices, go, 0)
        lax.fori_loop(1, devices, done, 0)

    exchange(lambda other: stat.at[other], stat_in, s1_send, s1_recv)
    stat_in[me] = stat[me]

    every = stat_in[...]
    tops, totals, picks = every[:, 0, :], every[:, 1, :], every[:, 2, :]
    row_top = jnp.max(tops, axis=0, keepdims=True)
    row_total = jnp.sum(totals * jnp.exp(tops - row_top), axis=0, keepdims=True)
    picked = jnp.sum(picks, axis=0, keepdims=True)
    inside = lax.broadcasted_iota(jnp.int32, (1, LANES), 1) < share
    valid = mask[...]
    raw = jnp.where(inside, jnp.log(jnp.where(inside, row_total, 1.0)) + row_top - picked, 0.0)
    loss = raw * valid
    loss_out[...] = loss

    def column(row):
        return jnp.transpose(jnp.broadcast_to(row, (LANES, LANES)))

    hot = dom[...] == lax.broadcasted_iota(jnp.int32, (LANES, LANES), 1)
    part[0:1, :] = jnp.sum(jnp.where(hot, column(loss), 0.0), axis=0, keepdims=True)
    part[1:2, :] = jnp.sum(jnp.where(hot, column(valid), 0.0), axis=0, keepdims=True)
    part[2:TILE, :] = jnp.zeros((TILE - 2, LANES), jnp.float32)
    exchange(lambda other: part, part_in, s2_send, s2_recv)
    part_in[me] = part[...]
    sums = jnp.sum(part_in[...], axis=0)
    mean_out[...] = sums[0:1, :] / jnp.maximum(sums[1:2, :], 1.0)

    for places, copy in sent:
        guarded(places, copy.wait_send)
    for copy in wsent:
        copy.wait_send()


def kernel_body(hidden, weight, targets, domains, seq_len):
    vocab = lax.axis_size("vocab")
    depth = vocab // 4
    devices = 2 * vocab
    tok_rows, kb = hidden.shape
    columns = weight.shape[1] // 2
    share = tok_rows // vocab
    valid, domain_share = token_share(domains, seq_len, share)
    valid = jnp.pad(valid, (0, LANES - share)).reshape(1, LANES)
    dom = jnp.broadcast_to(
        jnp.pad(domain_share, (0, LANES - share), constant_values=-1)[:, None], (LANES, LANES)
    )
    tgt = targets.reshape(tok_rows // LANES, LANES)
    steps = 4 * depth
    anywhere = pl.BlockSpec(memory_space=pl.ANY)
    vmem = pl.BlockSpec(memory_space=pltpu.VMEM)
    dma = pltpu.SemaphoreType.DMA
    loss, mean = pl.pallas_call(
        functools.partial(kernel, depth),
        out_shape=[jax.ShapeDtypeStruct((1, LANES), jnp.float32)] * 2,
        in_specs=[anywhere, anywhere, vmem, vmem, vmem],
        out_specs=[vmem, vmem],
        scratch_shapes=[
            pltpu.VMEM((2, vocab, tok_rows, kb), jnp.bfloat16),
            pltpu.VMEM((vocab, kb, columns), jnp.bfloat16),
            pltpu.VMEM((2 * tok_rows, columns), jnp.float32),
            pltpu.VMEM((2,) + tgt.shape, jnp.int32),
            pltpu.VMEM((2 * tok_rows, LANES), jnp.float32),
            pltpu.VMEM((devices, TILE, LANES), jnp.float32),
            pltpu.VMEM((devices, TILE, LANES), jnp.float32),
            pltpu.VMEM((TILE, LANES), jnp.float32),
            pltpu.VMEM((devices, TILE, LANES), jnp.float32),
            dma((2,)),
            dma((2, vocab)),
            dma((vocab,)),
            dma((steps, 6)),
            dma((vocab // 2,)),
            dma((2,)),
            dma((devices,)),
            dma((devices,)),
            dma((devices,)),
            dma((devices,)),
        ],
        compiler_params=pltpu.CompilerParams(
            collective_id=0, has_side_effects=True, vmem_limit_bytes=40 << 20
        ),
        cost_estimate=pl.CostEstimate(
            flops=4 * tok_rows * kb * vocab * columns, bytes_accessed=16 << 20, transcendentals=0
        ),
    )(hidden, weight, tgt, dom, valid)
    return loss[0, :share], mean[0, :DOMAINS]


def solution(mesh):
    tok, vocab = mesh.shape["tok"], mesh.shape["vocab"]

    def step(hidden, weight, targets, domains, seq_len):
        tok_rows = hidden.shape[0]
        fits = (
            tok == 2
            and vocab % 8 == 0
            and tok * tok_rows * weight.shape[0] * tok * 2 <= GATHER_LIMIT
            and tok_rows % (LANES * 2) == 0
            and tok_rows % (vocab * TILE) == 0
            and tok_rows // vocab <= LANES
            and weight.shape[1] % (2 * LANES) == 0
            and hidden.shape[1] % LANES == 0
        )
        chosen = kernel_body if fits else body
        return chosen(hidden, weight, targets, domains, seq_len)

    in_specs = (P("tok", "vocab"), P("tok", "vocab"), P("tok"), P("tok"), P("tok"))
    out_specs = (P(("tok", "vocab")), P())
    return jax.shard_map(step, mesh=mesh, in_specs=in_specs, out_specs=out_specs, check_vma=False)
```

time: 271 us -> 105 us (0.39)
  waiting for transfers between devices: 192 us -> 0 us
  Pallas kernels: 0 us -> 97.2 us
  blocking collectives: 38.2 us -> 0 us
  between operations: 14.1 us -> 0.66 us
  matrix products: 11.4 us -> 0 us
  starting transfers between devices: 10.4 us -> 0 us
  local copies, waits for them, and re-layouts: 2.8 us -> 5.74 us
    all_gather x2 -> x0, waiting for transfers between devices: 175 us -> none  [the longest x1 108 us: body(): lax.all_gather(weight, 'tok', axis=0, tiled=True)]
    pallas_call x0 -> x1, Pallas kernels: none -> 97.2 us  [kernel_body(): pl.pallas_call(functools.partial(kernel, depth), out_shape=[jax.ShapeDtyp...]
    psum x1 -> x0, blocking collectives: 38.2 us -> none  [body(): lax.psum((domain_sum, domain_count), ('tok', 'vocab'))]
    all_to_all x3 -> x0, waiting for transfers between devices: 15.8 us -> none  [the longest x1 6.14 us: body(): lax.all_to_all(sum_loc.reshape(groups, share_len), 'vocab', split_axis=0,...]
    dot_general x3 -> x0, matrix products: 11.4 us -> none  [the longest x1 11.1 us: body(): jnp.dot(features, lax.all_gather(weight, 'tok', axis=0, tiled=True), pref...]
    all_to_all x3 -> x0, starting transfers between devices: 10.3 us -> none  [the longest x1 3.49 us: body(): lax.all_to_all(picked_loc.reshape(groups, share_len), 'vocab', split_axis...]
    unnamed x6, local copies, waits for them, and re-layouts: 0.02 us -> 3.87 us
  transfers between devices with their start and end apart: 5 -> 0, of which waited for: 5 -> 0; matrix products, arithmetic and copies ran while one was open for 1% -> 0% of each run, Pallas kernels for 0% -> 0%
where the time goes in v1:
time: 105 us; the launch traced here: 104 us
  Pallas kernels  97.2 us (93%)
  local copies, waits for them, and re-layouts  5.74 us (5%)
    pallas_call x1, Pallas kernels, kernel_body(): pl.pallas_call(functools.partial(kernel, depth), out_shape=[jax.ShapeDtyp...  97.2 us
    unnamed x6, local copies, waits for them, and re-layouts  3.87 us

profile of v1, /device:TPU:0, one launch (start us, length us, event | category | flops | bytes accessed | tf_op | source)
XLA Modules:
  0.0 104.4 jit_solution(2918417629722047079)
XLA Ops:
  0.6 0.8 dynamic_slice.3
  1.4 0.7 select_reduce_fusion
  2.2 0.1 broadcast_in_dim.20.dom
  2.3 0.0 copy-start
  2.3 2.2 %copy-done = bf16[2048,1024]{1,0:T(8,128)(2,1)S(1)} copy-done((bf16[2048,1024]{1,0:T(8,128)(2,1)S(1)}, bf16[2048,1024]{1,0:T(8,128)(2,1)}, u32[]{:S(2)}) %copy-start) | copy-done | bytes 4194328
  4.5 0.0 copy-start.1
  4.5 1.0 copy-done.1
  5.5 0.0 copy-start.2
  5.5 0.7 copy-done.2
  6.1 97.2 %shard_map.68 = (f32[1,128]{1,0:T(1,128)S(1)}, f32[1,128]{1,0:T(1,128)S(1)}) custom-call(bf16[768,256]{1,0:T(8,128)(2,1)S(1)} %copy-done.1, bf16[2048,1024]{1,0:T(8,128)(2,1)S(1)} %copy-done, s32[6,128]{1,0:T(8,128)S(1)} %bitcast.7, s32[128,128]{1,0:T(8,128)S(1)} %broadcast_in_dim.20.dom, f32[1,128]{1,0:T(1,128)S(1)} %fusion.1.mask), custom_call_target="tpu_custom_call" | custom-call | flops 6442450944 | bytes 16777216 | tf_op jit(solution)/shard_map/pallas_call | solution.py:456
  103.4 0.5 slice_bitcast_fusion.1
  103.9 0.5 slice_bitcast_fusion
  (4 shorter events, 0.0 us)
Async XLA Ops:
  2.3 2.2 %copy-start = (bf16[2048,1024]{1,0:T(8,128)(2,1)S(1)}, bf16[2048,1024]{1,0:T(8,128)(2,1)}, u32[]{:S(2)}) copy-start(bf16[2048,1024]{1,0:T(8,128)(2,1)} %weight.1) | copy-start | bytes 12582916
  4.5 1.0 copy-start.1
  5.5 0.7 copy-start.2

commit v2 on v1

--- a/solution.py
+++ b/solution.py
@@ -12,6 +12,8 @@
 LANES = 128
 TILE = 8
 GATHER_LIMIT = 24 << 20
+PARTS = 2
+STATS = 4
 MESH = pl.DeviceIdType.MESH
 
 
@@ -75,22 +77,23 @@
     queues = {}
     have = [dict() for _ in range(depth)]
     for z in range(depth):
-        have[z][(0, 0, z)] = 0.0
-        have[z][(1, 0, z)] = 1.0
+        for h in range(PARTS):
+            have[z][(0, 0, z, h)] = 0.0
+            have[z][(1, 0, z, h)] = (h + 1.0) / PARTS
     pending = [(have[z][s], z, s) for z in range(depth) for s in have[z]]
     free = {}
     sends = [dict() for _ in range(depth)]
 
     def push(now, z, link, shard):
         start = max(now, free.get((z, link), 0.0))
-        free[(z, link)] = start + 1.0
+        free[(z, link)] = start + 1.0 / PARTS
         to, item = {
-            "y": (z, (shard[0], 1, shard[2])),
+            "y": (z, (shard[0], 1) + shard[2:]),
             "up": (z + 1, shard),
             "down": (z - 1, shard),
         }[link]
-        have[to][item] = start + 1.0
-        pending.append((start + 1.0, to, item))
+        have[to][item] = start + 1.0 / PARTS
+        pending.append((start + 1.0 / PARTS, to, item))
         sends[z].setdefault(shard, []).append(link)
 
     while pending:
@@ -107,15 +110,17 @@
             push(now, z, "y", shard)
     for z in range(depth):
         link = "up" if z % 2 == 0 else "down"
-        start = max(have[z][(0, 1, z)], free[(z, link)])
-        have[z ^ 1][(0, 1, z)] = start + 1.0
+        for h in range(PARTS):
+            start = max(have[z][(0, 1, z, h)], free[(z, link)])
+            free[(z, link)] = start + 1.0 / PARTS
+            have[z ^ 1][(0, 1, z, h)] = start + 1.0 / PARTS
     order = []
     for z in range(depth):
         link = "up" if z % 2 == 0 else "down"
         events = sorted((time, shard) for shard, time in have[z].items())
         after = max(
             [i for i, (_, s) in enumerate(events) if link in sends[z].get(s, ())]
-            + [i for i, (_, s) in enumerate(events) if s == (0, 1, z)]
+            + [i for i, (_, s) in enumerate(events) if s[:3] == (0, 1, z)]
         )
         rows = []
         for i, (time, shard) in enumerate(events):
@@ -142,27 +147,26 @@
             for zz in range(depth):
                 for dy in range(2):
                     for dc in range(2):
-                        time = max(arrival[(0, dy, zz)], arrival[(1, dy, zz)]) + 0.15 * dc
+                        time = max(a for s, a in arrival.items() if s[1:3] == (dy, zz)) + 0.15 * dc
                         ready.append((max(time, at.get((zz, dy, dc), 0.0)), (zz, dy, dc)))
             products[(t, z)] = sorted(ready)
     keys = sorted(products)
     count = len(order[0])
     steps = [
-        (sum(order[z][i][0] for z in range(depth)) / depth, 0, i) for i in range(1, count)
+        (sum(order[z][i][0] for z in range(depth)) / depth, 0, i) for i in range(PARTS, count)
     ]
     steps += [
         (sum(products[k][i][0] for k in keys) / len(keys) + 0.2, 1, i)
         for i in range(len(products[keys[0]]))
     ]
     steps.sort()
-    arrived = {z: {order[z][0][1]} for z in range(depth)}
+    arrived = {z: {order[z][i][1] for i in range(PARTS)} for z in range(depth)}
     sequence, waiting = [], []
 
     def ready_now(i):
         return all(
             products[k][i][1][2] == 1
-            or {(0,) + products[k][i][1][1::-1], (1,) + products[k][i][1][1::-1]}
-            <= arrived[k[1]]
+            or sum(s[1:3] == products[k][i][1][1::-1] for s in arrived[k[1]]) == 2 * PARTS
             for k in keys
         )
 
@@ -180,8 +184,8 @@
 
 
 def kernel(
-    depth, hid, weight, tgt, dom, mask, loss_out, mean_out,
-    held, wts, acc, tgt_all, tgt_col, stat, stat_in, part, part_in,
+    depth, hid, weight, tgt, dom, seq, loss_out, mean_out,
+    held, wts, turned, acc, tgt_all, dom_all, stat, stat_in, part, part_in,
     own_sem, held_sem, wts_sem, send_sem, wsend_sem, tgt_sem,
     s1_send, s1_recv, s2_send, s2_recv,
 ):
@@ -206,8 +210,15 @@
 
     key = t * depth + z
 
-    own = pltpu.make_async_copy(hid, held.at[t, v], own_sem.at[0])
-    own.start()
+    rows_of = tok_rows // PARTS
+    owns = [
+        pltpu.make_async_copy(hid.at[pl.ds(h * rows_of, rows_of)], held.at[t, v, h], own_sem.at[2 + h])
+        for h in range(PARTS)
+    ]
+    for own in owns:
+        own.start()
+    own_dom = pltpu.make_async_copy(dom, dom_all, own_sem.at[0])
+    own_dom.start()
     own_tgt = pltpu.make_async_copy(tgt, tgt_all.at[t], own_sem.at[1])
     own_tgt.start()
 
@@ -231,8 +242,10 @@
         return carry
 
     lax.fori_loop(1, devices, greet, 0)
-    own.wait()
+    for own in owns:
+        own.wait()
     own_tgt.wait()
+    own_dom.wait()
     pl.semaphore_wait(barrier, devices - 1)
 
     where = {
@@ -246,12 +259,12 @@
     lanes_of = {"x": 0, "y": 1, "up": 2, "down": 3, "far": 4, "pair": 5}
     sent = []
 
-    def send(tt, vv, link, step, places):
+    def send(tt, vv, h, link, step, places, lane=None):
         copy = pltpu.make_async_remote_copy(
-            src_ref=held.at[tt, vv],
-            dst_ref=held.at[tt, vv],
-            send_sem=send_sem.at[step, lanes_of[link]],
-            recv_sem=held_sem.at[tt, vv],
+            src_ref=held.at[tt, vv, h],
+            dst_ref=held.at[tt, vv, h],
+            send_sem=send_sem.at[step, lanes_of[link] if lane is None else lane],
+            recv_sem=held_sem.at[tt, vv, h],
             device_id=where[link](),
             device_id_type=MESH,
         )
@@ -272,20 +285,26 @@
         yy = (y + sel([order[p][step][1][1] for p in range(depth)], z)) % 2
         zz = sel([order[p][step][1][2] for p in range(depth)], z)
         vv = zz * 4 + yy * 2 + c
-        if step:
-            pltpu.make_async_copy(hid, held.at[tt, vv], held_sem.at[tt, vv]).wait()
-        if not step:
-            send(tt, vv, "x", 0, list(range(depth)))
+        h = sel([order[p][step][1][3] for p in range(depth)], z)
+        if step >= PARTS:
+            landed(tt, vv, h)
+        else:
+            send(tt, vv, h, "x", step, list(range(depth)))
         for link in ("up", "down", "y"):
             places = [p for p in range(depth) if link in order[p][step][2]]
             if places:
-                send(tt, vv, link, step, places)
-        send(tt, vv, "pair", step, list(range(depth)))
+                send(tt, vv, h, link, step, places)
+        send(tt, vv, h, "pair", step, list(range(depth)))
         places = [p for p in range(depth) if "far" in order[p][step][2]]
         if places:
-            send(t, z * 4 + (1 - y) * 2 + c, "far", step, places)
-
-    fan_out(0)
+            for part_ in range(PARTS):
+                send(t, z * 4 + (1 - y) * 2 + c, part_, "far", step, places, 6 + part_)
+
+    def landed(tt, vv, h):
+        pltpu.make_async_copy(held.at[tt, vv, h], held.at[tt, vv, h], held_sem.at[tt, vv, h]).wait()
+
+    for step in range(PARTS):
+        fan_out(step)
     tgt_copy = pltpu.make_async_remote_copy(
         src_ref=tgt_all.at[t], dst_ref=tgt_all.at[t],
         send_sem=tgt_sem.at[0], recv_sem=tgt_sem.at[1],
@@ -314,16 +333,6 @@
 
     tgt_copy.wait()
 
-    def spread(i, carry):
-        for h in range(2):
-            row = tgt_all[h, pl.ds(i, 1), :].astype(jnp.float32)
-            tgt_col[pl.ds(pl.multiple_of(h * tok_rows + i * LANES, LANES), LANES), :] = jnp.transpose(
-                jnp.broadcast_to(row, (LANES, LANES))
-            )
-        return carry
-
-    lax.fori_loop(0, tok_rows // LANES, spread, 0)
-
     def product(i, first):
         chunk = [products[(k // depth, k % depth)][i][1] for k in range(2 * depth)]
         zz = sel([ch[0] for ch in chunk], key)
@@ -333,7 +342,8 @@
 
         def wait_pair():
             for h in range(2):
-                pltpu.make_async_copy(hid, held.at[h, vv], held_sem.at[h, vv]).wait()
+                for part_ in range(PARTS):
+                    landed(h, vv, part_)
 
         if isinstance(dc, int):
             if dc:
@@ -341,20 +351,21 @@
         else:
             pl.when(dc == 1)(wait_pair)
         pltpu.make_async_copy(wts.at[vv], wts.at[vv], wts_sem.at[vv]).wait()
-        step_rows = 256 if tok_rows % 256 == 0 else LANES
+        turned[...] = jnp.transpose(wts[vv])
 
         def tile(r, carry):
-            for h in range(2):
-                at = pl.ds(pl.multiple_of(r * step_rows, step_rows), step_rows)
-                to = pl.ds(pl.multiple_of(h * tok_rows + r * step_rows, step_rows), step_rows)
-                got = jnp.dot(held[h, vv, at, :], wts[vv], preferred_element_type=jnp.float32)
-                if first:
-                    acc[to, :] = got
-                else:
-                    acc[to, :] += got
+            to = pl.ds(pl.multiple_of(r * rows_of, LANES), rows_of)
+            got = lax.dot_general(
+                turned[...], held[r // PARTS, vv, r % PARTS], (((1,), (1,)), ((), ())),
+                preferred_element_type=jnp.float32,
+            )
+            if first:
+                acc[:, to] = got
+            else:
+                acc[:, to] += got
             return carry
 
-        lax.fori_loop(0, tok_rows // step_rows, tile, 0)
+        lax.fori_loop(0, 2 * PARTS, tile, 0)
 
     first = True
     for kind, i in sequence:
@@ -365,22 +376,22 @@
             first = False
 
     first_col = (v * 2 + t) * cols
-    lane = lax.broadcasted_iota(jnp.int32, (share, LANES), 1)
-    col = lax.broadcasted_iota(jnp.int32, (share, cols), 1)
-
-    def finish(w, carry):
-        rows = pl.ds(pl.multiple_of(w * share, share), share)
-        got = acc[rows, :]
-        wanted = tgt_col[rows, 0:1].astype(jnp.int32) - first_col
-        top = jnp.max(got, axis=1, keepdims=True)
-        total = jnp.sum(jnp.exp(got - top), axis=1, keepdims=True)
-        picked = jnp.sum(jnp.where(col == wanted, got, 0.0), axis=1, keepdims=True)
-        both = jnp.where(lane == 0, top, jnp.where(lane == 1, total, picked))
-        both = jnp.concatenate([both, jnp.zeros((LANES - share, LANES), jnp.float32)], axis=0)
-        stat[w] = jnp.transpose(both)[:TILE, :]
+    tiles = tok_rows // LANES
+    col = lax.broadcasted_iota(jnp.int32, (cols, LANES), 0)
+
+    def finish(b, carry):
+        got = acc[:, pl.ds(pl.multiple_of(b * LANES, LANES), LANES)]
+        wanted = tgt_all[b // tiles, pl.ds(b % tiles, 1), :] - first_col
+        top = jnp.max(got, axis=0, keepdims=True)
+        total = jnp.sum(jnp.exp(got - top), axis=0, keepdims=True)
+        picked = jnp.sum(jnp.where(col == wanted, got, 0.0), axis=0, keepdims=True)
+        stat[b] = jnp.concatenate([top, total, picked, picked], axis=0)
         return carry
 
-    lax.fori_loop(0, devices, finish, 0)
+    lax.fori_loop(0, 2 * tiles, finish, 0)
+
+    def first_tile(vv):
+        return jnp.minimum(vv * share // LANES, tiles - 2)
 
     def exchange(src_at, dst, send, recv):
         def copy(k):
@@ -404,27 +415,33 @@
         lax.fori_loop(1, devices, go, 0)
         lax.fori_loop(1, devices, done, 0)
 
-    exchange(lambda other: stat.at[other], stat_in, s1_send, s1_recv)
-    stat_in[me] = stat[me]
-
-    every = stat_in[...]
-    tops, totals, picks = every[:, 0, :], every[:, 1, :], every[:, 2, :]
-    row_top = jnp.max(tops, axis=0, keepdims=True)
-    row_total = jnp.sum(totals * jnp.exp(tops - row_top), axis=0, keepdims=True)
-    picked = jnp.sum(picks, axis=0, keepdims=True)
-    inside = lax.broadcasted_iota(jnp.int32, (1, LANES), 1) < share
-    valid = mask[...]
-    raw = jnp.where(inside, jnp.log(jnp.where(inside, row_total, 1.0)) + row_top - picked, 0.0)
-    loss = raw * valid
-    loss_out[...] = loss
+    def window(other):
+        return pl.ds(other // vocab * tiles + first_tile(other % vocab), 2)
+
+    exchange(lambda other: stat.at[window(other)], stat_in, s1_send, s1_recv)
+    stat_in[me] = stat[window(me)]
 
     def column(row):
         return jnp.transpose(jnp.broadcast_to(row, (LANES, LANES)))
 
-    hot = dom[...] == lax.broadcasted_iota(jnp.int32, (LANES, LANES), 1)
-    part[0:1, :] = jnp.sum(jnp.where(hot, column(loss), 0.0), axis=0, keepdims=True)
-    part[1:2, :] = jnp.sum(jnp.where(hot, column(valid), 0.0), axis=0, keepdims=True)
-    part[2:TILE, :] = jnp.zeros((TILE - 2, LANES), jnp.float32)
+    tile0 = first_tile(v)
+    lane = lax.broadcasted_iota(jnp.int32, (1, LANES), 1)
+    classes = lax.broadcasted_iota(jnp.int32, (LANES, LANES), 1).astype(jnp.float32)
+    sums, counts = jnp.zeros((1, LANES), jnp.float32), jnp.zeros((1, LANES), jnp.float32)
+    for j in range(2):
+        tops, totals, picks = (stat_in[:, j, row, :] for row in range(3))
+        row_top = jnp.max(tops, axis=0, keepdims=True)
+        row_total = jnp.sum(totals * jnp.exp(tops - row_top), axis=0, keepdims=True)
+        picked = jnp.sum(picks, axis=0, keepdims=True)
+        position = (tile0 + j) * LANES + lane
+        inside = jnp.logical_and(position >= v * share, position < (v + 1) * share)
+        valid = jnp.where(inside, (lane < seq[tile0 + j]).astype(jnp.float32), 0.0)
+        loss = (jnp.log(row_total) + row_top - picked) * valid
+        loss_out[j : j + 1, :] = loss
+        hot = column(dom_all[pl.ds(tile0 + j, 1), :].astype(jnp.float32)) == classes
+        sums += jnp.sum(jnp.where(hot, column(loss), 0.0), axis=0, keepdims=True)
+        counts += jnp.sum(jnp.where(hot, column(valid), 0.0), axis=0, keepdims=True)
+    part[...] = jnp.concatenate([sums, counts], axis=0)
     exchange(lambda other: part, part_in, s2_send, s2_recv)
     part_in[me] = part[...]
     sums = jnp.sum(part_in[...], axis=0)
@@ -443,35 +460,33 @@
     tok_rows, kb = hidden.shape
     columns = weight.shape[1] // 2
     share = tok_rows // vocab
-    valid, domain_share = token_share(domains, seq_len, share)
-    valid = jnp.pad(valid, (0, LANES - share)).reshape(1, LANES)
-    dom = jnp.broadcast_to(
-        jnp.pad(domain_share, (0, LANES - share), constant_values=-1)[:, None], (LANES, LANES)
-    )
-    tgt = targets.reshape(tok_rows // LANES, LANES)
-    steps = 4 * depth
+    tiles = tok_rows // LANES
     anywhere = pl.BlockSpec(memory_space=pl.ANY)
     vmem = pl.BlockSpec(memory_space=pltpu.VMEM)
     dma = pltpu.SemaphoreType.DMA
     loss, mean = pl.pallas_call(
         functools.partial(kernel, depth),
-        out_shape=[jax.ShapeDtypeStruct((1, LANES), jnp.float32)] * 2,
-        in_specs=[anywhere, anywhere, vmem, vmem, vmem],
+        out_shape=[
+            jax.ShapeDtypeStruct((2, LANES), jnp.float32),
+            jax.ShapeDtypeStruct((1, LANES), jnp.float32),
+        ],
+        in_specs=[anywhere] * 4 + [pl.BlockSpec(memory_space=pltpu.SMEM)],
         out_specs=[vmem, vmem],
         scratch_shapes=[
-            pltpu.VMEM((2, vocab, tok_rows, kb), jnp.bfloat16),
+            pltpu.VMEM((2, vocab, PARTS, tok_rows // PARTS, kb), jnp.bfloat16),
             pltpu.VMEM((vocab, kb, columns), jnp.bfloat16),
-            pltpu.VMEM((2 * tok_rows, columns), jnp.float32),
-            pltpu.VMEM((2,) + tgt.shape, jnp.int32),
-            pltpu.VMEM((2 * tok_rows, LANES), jnp.float32),
-            pltpu.VMEM((devices, TILE, LANES), jnp.float32),
-            pltpu.VMEM((devices, TILE, LANES), jnp.float32),
-            pltpu.VMEM((TILE, LANES), jnp.float32),
-            pltpu.VMEM((devices, TILE, LANES), jnp.float32),
-            dma((2,)),
-            dma((2, vocab)),
+            pltpu.VMEM((columns, kb), jnp.bfloat16),
+            pltpu.VMEM((columns, 2 * tok_rows), jnp.float32),
+            pltpu.VMEM((2, tiles, LANES), jnp.int32),
+            pltpu.VMEM((tiles, LANES), jnp.int32),
+            pltpu.VMEM((2 * tiles, STATS, LANES), jnp.float32),
+            pltpu.VMEM((devices, 2, STATS, LANES), jnp.float32),
+            pltpu.VMEM((2, LANES), jnp.float32),
+            pltpu.VMEM((devices, 2, LANES), jnp.float32),
+            dma((2 + PARTS,)),
+            dma((2, vocab, PARTS)),
             dma((vocab,)),
-            dma((steps, 6)),
+            dma((4 * depth * PARTS, 6 + PARTS)),
             dma((vocab // 2,)),
             dma((2,)),
             dma((devices,)),
@@ -480,13 +495,17 @@
             dma((devices,)),
         ],
         compiler_params=pltpu.CompilerParams(
-            collective_id=0, has_side_effects=True, vmem_limit_bytes=40 << 20
+            collective_id=0, has_side_effects=True, vmem_limit_bytes=60 * 1024 * 1024
         ),
         cost_estimate=pl.CostEstimate(
             flops=4 * tok_rows * kb * vocab * columns, bytes_accessed=16 << 20, transcendentals=0
         ),
-    )(hidden, weight, tgt, dom, valid)
-    return loss[0, :share], mean[0, :DOMAINS]
+    )(
+        hidden, weight, targets.reshape(tiles, LANES), domains.reshape(tiles, LANES), seq_len
+    )
+    start = lax.axis_index("vocab") * share
+    start = start - jnp.minimum(start // LANES, tiles - 2) * LANES
+    return lax.dynamic_slice_in_dim(loss.reshape(2 * LANES), start, share), mean[0, :DOMAINS]
 
 
 def solution(mesh):
@@ -498,7 +517,8 @@
             tok == 2
             and vocab % 8 == 0
             and tok * tok_rows * weight.shape[0] * tok * 2 <= GATHER_LIMIT
-            and tok_rows % (LANES * 2) == 0
+            and tok_rows % (LANES * PARTS) == 0
+            and SEQ_LEN == LANES
             and tok_rows % (vocab * TILE) == 0
             and tok_rows // vocab <= LANES
             and weight.shape[1] % (2 * LANES) == 0

time: 105 us -> 96.3 us (0.917)
  Pallas kernels: 97.2 us -> 93.1 us
  local copies, waits for them, and re-layouts: 5.74 us -> 2.39 us
    pallas_call x1, Pallas kernels: 97.2 us -> 93.1 us  [kernel_body(): pl.pallas_call(functools.partial(kernel, depth), out_shape=[jax.ShapeDtyp...]
    unnamed x6 -> x0, local copies, waits for them, and re-layouts: 3.87 us -> none
where the time goes in v2:
time: 96.3 us; the launch traced here: 96.1 us
  Pallas kernels  93.1 us (97%)
  local copies, waits for them, and re-layouts  2.39 us (2%)
    pallas_call x1, Pallas kernels, kernel_body(): pl.pallas_call(functools.partial(kernel, depth), out_shape=[jax.ShapeDtyp...  93.1 us

profile of v2, /device:TPU:0, one launch (start us, length us, event | category | flops | bytes accessed | tf_op | source)
XLA Modules:
  0.0 96.1 jit_solution(17571421108118052972)
XLA Ops:
  0.7 93.1 %shard_map.68 = (f32[2,128]{1,0:T(2,128)}, f32[1,128]{1,0:T(1,128)}) custom-call(bf16[768,256]{1,0:T(8,128)(2,1)} %hid.1, bf16[2048,1024]{1,0:T(8,128)(2,1)} %weight.1, s32[6,128]{1,0:T(8,128)} %bitcast.5, s32[6,128]{1,0:T(8,128)} %bitcast.6, s32[6]{0:T(128)} %seq.1), custom_call_target="tpu_custom_call" | custom-call | flops 6442450944 | bytes 16777216 | tf_op jit(solution)/shard_map/pallas_call | solution.py:467
  93.8 1.2 %dynamic_slice.3 = f32[48]{0:T(128)} dynamic-slice(f32[256]{0:T(256)} %bitcast.7, s32[]{:T(128)S(6)} %select_n.9), dynamic_slice_sizes={48} | dynamic-slice | bytes 388 | tf_op jit(solution)/shard_map/dynamic_slice | solution.py:508
  95.0 1.1 %slice_bitcast_fusion = f32[64]{0:T(128)} fusion(f32[1,128]{1,0:T(1,128)} %get-tuple-element.5), kind=kLoop, calls=%fused_computation | loop fusion | bytes 512 | tf_op jit(solution)/shard_map/squeeze | solution.py:508

commit v3 on v2

--- a/solution.py
+++ b/solution.py
@@ -12,7 +12,7 @@
 LANES = 128
 TILE = 8
 GATHER_LIMIT = 24 << 20
-PARTS = 2
+PARTS = 1
 STATS = 4
 MESH = pl.DeviceIdType.MESH
 
@@ -183,6 +183,15 @@
     return order, weight_order, products, sequence
 
 
+def count_sends(depth):
+    order = plan(depth)
+    total = PARTS + len(order[0])
+    for step in range(len(order[0])):
+        links = {link for rows in order for link in rows[step][2]}
+        total += len(links - {"far"}) + PARTS * ("far" in links)
+    return total
+
+
 def kernel(
     depth, hid, weight, tgt, dom, seq, loss_out, mean_out,
     held, wts, turned, acc, tgt_all, dom_all, stat, stat_in, part, part_in,
@@ -256,14 +265,13 @@
         "far": lambda: (t, v + 4 - 8 * (z % 2)),
         "pair": lambda: (t, v + 1 - 2 * c),
     }
-    lanes_of = {"x": 0, "y": 1, "up": 2, "down": 3, "far": 4, "pair": 5}
     sent = []
 
-    def send(tt, vv, h, link, step, places, lane=None):
+    def send(tt, vv, h, link, places):
         copy = pltpu.make_async_remote_copy(
             src_ref=held.at[tt, vv, h],
             dst_ref=held.at[tt, vv, h],
-            send_sem=send_sem.at[step, lanes_of[link] if lane is None else lane],
+            send_sem=send_sem.at[len(sent)],
             recv_sem=held_sem.at[tt, vv, h],
             device_id=where[link](),
             device_id_type=MESH,
@@ -289,16 +297,16 @@
         if step >= PARTS:
             landed(tt, vv, h)
         else:
-            send(tt, vv, h, "x", step, list(range(depth)))
+            send(tt, vv, h, "x", list(range(depth)))
         for link in ("up", "down", "y"):
             places = [p for p in range(depth) if link in order[p][step][2]]
             if places:
-                send(tt, vv, h, link, step, places)
-        send(tt, vv, h, "pair", step, list(range(depth)))
+                send(tt, vv, h, link, places)
+        send(tt, vv, h, "pair", list(range(depth)))
         places = [p for p in range(depth) if "far" in order[p][step][2]]
         if places:
             for part_ in range(PARTS):
-                send(t, z * 4 + (1 - y) * 2 + c, part_, "far", step, places, 6 + part_)
+                send(t, z * 4 + (1 - y) * 2 + c, part_, "far", places)
 
     def landed(tt, vv, h):
         pltpu.make_async_copy(held.at[tt, vv, h], held.at[tt, vv, h], held_sem.at[tt, vv, h]).wait()
@@ -398,7 +406,7 @@
             other = (me + k) % devices
             return pltpu.make_async_remote_copy(
                 src_ref=src_at(other), dst_ref=dst.at[me],
-                send_sem=send.at[other], recv_sem=recv.at[me],
+                send_sem=send.at[0], recv_sem=recv.at[0],
                 device_id=(other // vocab, other % vocab), device_id_type=MESH,
             )
 
@@ -406,14 +414,10 @@
             copy(k).start()
             return carry
 
-        def done(k, carry):
-            other = (me + k) % devices
-            copy(k).wait_send()
-            pltpu.make_async_copy(dst.at[other], dst.at[other], recv.at[other]).wait()
-            return carry
-
         lax.fori_loop(1, devices, go, 0)
-        lax.fori_loop(1, devices, done, 0)
+        others = dst.at[pl.ds(0, devices - 1)]
+        pltpu.make_async_copy(others, others, send.at[0]).wait()
+        pltpu.make_async_copy(others, others, recv.at[0]).wait()
 
     def window(other):
         return pl.ds(other // vocab * tiles + first_tile(other % vocab), 2)
@@ -486,13 +490,13 @@
             dma((2 + PARTS,)),
             dma((2, vocab, PARTS)),
             dma((vocab,)),
-            dma((4 * depth * PARTS, 6 + PARTS)),
+            dma((count_sends(depth),)),
             dma((vocab // 2,)),
             dma((2,)),
-            dma((devices,)),
-            dma((devices,)),
-            dma((devices,)),
-            dma((devices,)),
+            dma((1,)),
+            dma((1,)),
+            dma((1,)),
+            dma((1,)),
         ],
         compiler_params=pltpu.CompilerParams(
             collective_id=0, has_side_effects=True, vmem_limit_bytes=60 * 1024 * 1024

time: 96.3 us -> 93 us (0.966)
  Pallas kernels: 93.1 us -> 89.8 us
    pallas_call x1, Pallas kernels: 93.1 us -> 89.8 us  [kernel_body(): pl.pallas_call(functools.partial(kernel, depth), out_shape=[jax.ShapeDtyp...]
where the time goes in v3:
time: 93 us; the launch traced here: 92.9 us
  Pallas kernels  89.8 us (97%)
  local copies, waits for them, and re-layouts  2.39 us (3%)
    pallas_call x1, Pallas kernels, kernel_body(): pl.pallas_call(functools.partial(kernel, depth), out_shape=[jax.ShapeDtyp...  89.8 us

profile of v3, /device:TPU:0, one launch (start us, length us, event | category | flops | bytes accessed | tf_op | source)
XLA Modules:
  0.0 92.9 jit_solution(15602245895069394251)
XLA Ops:
  0.7 89.8 %shard_map.68 = (f32[2,128]{1,0:T(2,128)}, f32[1,128]{1,0:T(1,128)}) custom-call(bf16[768,256]{1,0:T(8,128)(2,1)} %hid.1, bf16[2048,1024]{1,0:T(8,128)(2,1)} %weight.1, s32[6,128]{1,0:T(8,128)} %bitcast.5, s32[6,128]{1,0:T(8,128)} %bitcast.6, s32[6]{0:T(128)} %seq.1), custom_call_target="tpu_custom_call" | custom-call | flops 6442450944 | bytes 16777216 | tf_op jit(solution)/shard_map/pallas_call | solution.py:471
  90.5 1.2 %dynamic_slice.3 = f32[48]{0:T(128)} dynamic-slice(f32[256]{0:T(256)} %bitcast.7, s32[]{:T(128)S(6)} %select_n.9), dynamic_slice_sizes={48} | dynamic-slice | bytes 388 | tf_op jit(solution)/shard_map/dynamic_slice | solution.py:512
  91.7 1.1 %slice_bitcast_fusion = f32[64]{0:T(128)} fusion(f32[1,128]{1,0:T(1,128)} %get-tuple-element.5), kind=kLoop, calls=%fused_computation | loop fusion | bytes 512 | tf_op jit(solution)/shard_map/squeeze | solution.py:512
